TPU v7x, 32 devices: a whole 2x2x4 slice. The times are simulated.
32 devices in a mesh: rows: 8 (over z, y), rank: 4 (over x, core).
Axes of the slice: x: 2, y: 2, z: 4, core: 2. Of those that a mesh axis runs over, the one named last changes fastest.
Arguments:
- left_factor: bfloat16 [128, 16384], P(None, 'rows'), may hold values from -8 to 8
- right_factor: bfloat16 [128, 16384], P(None, 'rows'), may hold values from -8 to 8
- left_plan: float32 [256, 16384], P('rank', 'rows'), may hold values from 0.0068 to 147, as said below
- right_plan: float32 [256, 16384], P('rank', 'rows'), may hold values from 0.0068 to 147, as said below
- log_inner: float32 [256], P('rank'), may hold values from -1 to 1
- left_mass: float32 [16384], P('rows'), may hold values from 32 to 1024, as said below
- right_mass: float32 [16384], P('rows'), may hold values from 32 to 1024, as said below
Outputs:
- new_left: float32 [256, 16384], P('rank', 'rows')
- new_right: float32 [256, 16384], P('rank', 'rows')
- new_log_inner: float32 [256], P('rank')
Inputs may be any that keep to these rules, and one draw needn't show every extreme that they name: `left_plan`: positive entries. `right_plan`: positive entries. `left_mass`: positive point masses. `right_mass`: positive point masses.
All inputs are finite; a program needn't handle non-finite values. Where the computation divides by a largest or mean magnitude, that divisor is 1e-20 or more.
Results may differ from a plain program's by a relative error of at most 0.00045.
Values sent between devices are 32-bit elements; how exact they have to be, the bound alone decides.
A program may use at most 64 MiB of HBM per device.

v0:
```python
import jax
import jax.numpy as jnp
from jax import lax
from jax.sharding import PartitionSpec as P

RANK = 256
ITERS = 3


def contract_points(factor, plan):
    return lax.dot_general(
        factor, plan, (((1,), (1,)), ((), ())), preferred_element_type=jnp.float32
    )


def expand_points(projected, factor):
    return lax.dot_general(
        projected, factor, (((0,), (0,)), ((), ())), preferred_element_type=jnp.float32
    )


def balance(inner_mass, col_scale_left, col_total_left, col_scale_right, col_total_right):
    mixed = (
        jnp.log(inner_mass)
        + jnp.log(col_scale_left * col_total_left)
        + jnp.log(col_scale_right * col_total_right)
    )
    inner_mass = jnp.exp(mixed / 3.0)
    return (inner_mass, inner_mass / col_total_left, inner_mass / col_total_right)


def per_device(left_factor, right_factor, left_plan, right_plan, log_inner, left_mass, right_mass):
    precise = lax.Precision.HIGHEST
    columns = left_plan.shape[0]
    left_round = left_plan.astype(jnp.bfloat16)
    right_round = right_plan.astype(jnp.bfloat16)
    proj_right, proj_left, total_left, total_right = lax.psum(
        (
            contract_points(right_factor, right_round),
            contract_points(left_factor, left_round),
            jnp.sum(left_mass),
            jnp.sum(right_mass),
        ),
        "rows",
    )
    inner_mass = total_left / RANK * jnp.exp(log_inner)
    scaled_right = (proj_right / inner_mass[None, :]).astype(jnp.bfloat16)
    scaled_left = (proj_left / inner_mass[None, :]).astype(jnp.bfloat16)
    grad_left = expand_points(scaled_right, left_factor)
    grad_right = expand_points(scaled_left, right_factor)
    pairing = lax.psum(jnp.sum(left_round.astype(jnp.float32) * grad_left, axis=1), "rows")
    grad_inner = -pairing / inner_mass
    local_top = jnp.maximum(
        jnp.maximum(jnp.max(jnp.abs(grad_left)), jnp.max(jnp.abs(grad_right))),
        jnp.max(jnp.abs(grad_inner)),
    )
    largest = lax.pmax(local_top, ("rows", "rank"))
    step_size = 5.0 / jnp.maximum(largest, 0.25)
    tilted_left = left_plan * jnp.exp(-step_size * grad_left)
    tilted_right = right_plan * jnp.exp(-step_size * grad_right)
    inner_mass = inner_mass * jnp.exp(-step_size * grad_inner)
    right_norm = right_mass * (total_left / total_right)
    row_scale_left = left_mass
    row_scale_right = right_norm
    own_left = jnp.ones((columns,), jnp.float32)
    own_right = jnp.ones((columns,), jnp.float32)
    own_inner = inner_mass
    for repeat in range(ITERS):
        rows_left, rows_right = lax.psum(
            (
                jnp.dot(own_left, tilted_left, precision=precise),
                jnp.dot(own_right, tilted_right, precision=precise),
            ),
            "rank",
        )
        row_scale_left = left_mass / rows_left
        row_scale_right = right_norm / rows_right
        col_total_left, col_total_right = lax.psum(
            (
                jnp.dot(tilted_left, row_scale_left, precision=precise),
                jnp.dot(tilted_right, row_scale_right, precision=precise),
            ),
            "rows",
        )
        own_inner, own_left, own_right = balance(
            own_inner, own_left, col_total_left, own_right, col_total_right
        )
    new_left = row_scale_left[None, :] * tilted_left * own_left[:, None]
    new_right = row_scale_right[None, :] * tilted_right * own_right[:, None]
    new_log_inner = jnp.log(own_inner) - jnp.log(total_left / RANK)
    return (new_left, new_right, new_log_inner)


def solution(mesh):
    in_specs = (
        P(None, "rows"),
        P(None, "rows"),
        P("rank", "rows"),
        P("rank", "rows"),
        P("rank"),
        P("rows"),
        P("rows"),
    )
    out_specs = (P("rank", "rows"), P("rank", "rows"), P("rank"))
    return jax.shard_map(
        per_device, mesh=mesh, in_specs=in_specs, out_specs=out_specs, check_vma=False
    )
```

profile of v0, /device:TPU:0, one launch (start us, length us, event | category | flops | bytes accessed | tf_op | source)
XLA Modules:
  0.0 222.6 jit_solution(15531989773435869686)
XLA Ops:
  0.7 1.4 reduce_sum.29
  2.1 0.6 reduce_sum.27
  2.7 1.4 fusion.2
  4.5 40.8 %all-reduce.4 = (f32[128,64]{1,0:T(8,128)S(1)}, f32[]{:T(128)}) all-reduce(f32[128,64]{1,0:T(8,128)S(1)} %fusion, f32[]{:T(128)} %reduce_sum.27), channel_id=1, replica_groups=mesh['rows'=8,'rank'=4] {'rows'}, use_global_device_ids=true, to_apply=%region_2.0 | all-reduce | flops 8193 | bytes 65544 | tf_op jit(solution)/shard_map/psum | solution.py:37
  46.0 0.6 copy-done.6
  46.6 1.7 multiply_reduce_fusion
  48.3 34.9 %all-reduce.3 = (f32[128,64]{1,0:T(8,128)S(1)}, f32[64]{0:T(128)S(1)}, f32[]{:T(128)}) all-reduce(f32[128,64]{1,0:T(8,128)S(1)} %fusion.2, f32[64]{0:T(128)S(1)} %get-tuple-element.3, f32[]{:T(128)} %reduce_sum.29), channel_id=1, replica_groups=mesh['rows'=8,'rank'=4] {'rows'}, use_global_device_ids=true, to_apply=%region_4.0 | all-reduce | flops 8257 | bytes 66056 | tf_op jit(solution)/shard_map/psum | solution.py:37
  84.5 0.7 abs_reduce_fusion.2
  85.2 0.9 abs_reduce_fusion
  88.1 36.8 %pmax.7 = f32[]{:T(128)} all-reduce(f32[]{:T(128)S(6)} %max.12), channel_id=1, replica_groups=mesh['rows'=8,'rank'=4] {'rows','rank'}, use_global_device_ids=true, to_apply=%region_9.0 | all-reduce | flops 1 | bytes 8 | tf_op jit(solution)/shard_map/pmax | solution.py:57
  125.6 1.2 exponential_multiply_fusion
  126.8 0.4 fusion.16
  127.2 0.4 fusion.18
  127.5 11.1 %all-reduce.7 = (f32[2048]{0:T(1024)S(1)}, f32[2048]{0:T(1024)S(1)}) all-reduce(f32[2048]{0:T(1024)S(1)} %bitcast.64, f32[2048]{0:T(1024)S(1)} %bitcast.65), channel_id=1, replica_groups=mesh['rows'=8,'rank'=4] {'rank'}, use_global_device_ids=true, to_apply=%region_14.0 | all-reduce | flops 4096 | bytes 32768 | tf_op jit(solution)/shard_map/psum | solution.py:69
  138.7 0.5 convolution_bitcast_fusion.4
  139.2 0.5 convolution_bitcast_fusion.5
  139.7 20.3 %all-reduce.2 = (f32[64]{0:T(128)S(1)}, f32[64]{0:T(128)S(1)}) all-reduce(f32[64]{0:T(128)S(1)} %convolution_bitcast_fusion.4, f32[64]{0:T(128)S(1)} %convolution_bitcast_fusion.5), channel_id=1, replica_groups=mesh['rows'=8,'rank'=4] {'rows'}, use_global_device_ids=true, to_apply=%region_15.0 | all-reduce | flops 128 | bytes 1024 | tf_op jit(solution)/shard_map/psum | solution.py:78
  160.1 0.4 fusion.12
  160.5 0.4 fusion.14
  160.8 10.1 %all-reduce.6 = (f32[2048]{0:T(1024)S(1)}, f32[2048]{0:T(1024)S(1)}) all-reduce(f32[2048]{0:T(1024)S(1)} %bitcast.66, f32[2048]{0:T(1024)S(1)} %bitcast.67), channel_id=1, replica_groups=mesh['rows'=8,'rank'=4] {'rank'}, use_global_device_ids=true, to_apply=%region_18.0 | all-reduce | flops 4096 | bytes 32768 | tf_op jit(solution)/shard_map/psum | solution.py:69
  171.0 0.5 convolution_bitcast_fusion.2
  171.5 0.5 convolution_bitcast_fusion.3
  172.0 17.1 %all-reduce.1 = (f32[64]{0:T(128)S(1)}, f32[64]{0:T(128)S(1)}) all-reduce(f32[64]{0:T(128)S(1)} %convolution_bitcast_fusion.2, f32[64]{0:T(128)S(1)} %convolution_bitcast_fusion.3), channel_id=1, replica_groups=mesh['rows'=8,'rank'=4] {'rows'}, use_global_device_ids=true, to_apply=%region_19.0 | all-reduce | flops 128 | bytes 1024 | tf_op jit(solution)/shard_map/psum | solution.py:78
  189.2 0.4 fusion.8
  189.6 0.4 fusion.10
  189.9 10.1 %all-reduce.5 = (f32[2048]{0:T(1024)S(1)}, f32[2048]{0:T(1024)S(1)}) all-reduce(f32[2048]{0:T(1024)S(1)} %bitcast.68, f32[2048]{0:T(1024)S(1)} %bitcast.69), channel_id=1, replica_groups=mesh['rows'=8,'rank'=4] {'rank'}, use_global_device_ids=true, to_apply=%region_22.0 | all-reduce | flops 4096 | bytes 32768 | tf_op jit(solution)/shard_map/psum | solution.py:69
  200.1 0.5 convolution_bitcast_fusion
  200.6 0.5 convolution_bitcast_fusion.1
  201.1 19.1 %all-reduce = (f32[64]{0:T(128)S(1)}, f32[64]{0:T(128)S(1)}) all-reduce(f32[64]{0:T(128)S(1)} %convolution_bitcast_fusion, f32[64]{0:T(128)S(1)} %convolution_bitcast_fusion.1), channel_id=1, replica_groups=mesh['rows'=8,'rank'=4] {'rows'}, use_global_device_ids=true, to_apply=%region_23.0 | all-reduce | flops 128 | bytes 1024 | tf_op jit(solution)/shard_map/psum | solution.py:78
  220.3 0.5 log_subtract_fusion
  220.8 0.9 multiply_multiply_fusion.1
  221.7 0.9 multiply_multiply_fusion
  (26 shorter events, 0.4 us)
Async XLA Ops:
  0.6 2.1 copy-start
  0.6 1.5 copy-start.5
  2.7 1.4 copy-start.2
  2.7 1.4 copy-start.3
  4.2 42.5 %copy-start.1 = (f32[64,2048]{1,0:T(8,128)S(1)}, f32[64,2048]{1,0:T(8,128)}, u32[]{:S(2)}) copy-start(f32[64,2048]{1,0:T(8,128)} %param.9) | copy-start | bytes 1572868
  46.0 0.7 copy-start.6
  127.5 11.1 %copy-start.4 = (f32[2048]{0:T(1024)S(1)}, f32[2048]{0:T(1024)}, u32[]{:S(2)}) copy-start(f32[2048]{0:T(1024)} %param.13) | copy-start | bytes 24580
where the time goes:
time: 223 us
  blocking collectives  201 us (90%)
  matrix products  9.56 us (4%)
  other arithmetic  6.36 us (3%)
  between operations  5.5 us (2%)
    psum x2, blocking collectives, per_device(): lax.psum((contract_points(right_factor, right_round), contract_points(lef...  75.7 us
    psum x3, blocking collectives, per_device(): lax.psum((jnp.dot(tilted_left, row_scale_left, precision=precise), jnp.do...  56.6 us
    pmax x1, blocking collectives, per_device(): largest = lax.pmax(local_top, ('rows', 'rank'))  36.8 us
    psum x3, blocking collectives, per_device(): lax.psum((jnp.dot(own_left, tilted_left, precision=precise), jnp.dot(own_...  31.4 us

commit v1 on v0

v1 whole, which is shorter than its diff:
```python
import functools

import jax
import jax.numpy as jnp
from jax import lax
from jax.experimental import pallas as pl
from jax.experimental.pallas import tpu as pltpu
from jax.sharding import PartitionSpec as P

ITERS = 3
LANES = 128
UNROLL = 32
MESH = pl.DeviceIdType.MESH


def each(start, stop, body):
    if stop - start <= UNROLL:
        for index in range(start, stop):
            body(index)
    else:
        pl.loop(start, stop)(body)


def to_columns(row):
    return jnp.broadcast_to(row, (LANES, row.shape[1])).T


def kernel(
    n_rows, n_rank,
    lf_hbm, rf_hbm, lp_hbm, rp_hbm, log_ref, lm_ref, rm_ref,
    tl_hbm, tr_hbm, scale_ref, col_ref, log_out,
    lf, rf, lp, rp, tilt, log_row,
    part, parts, chunk, proj, totals, tops, sums, cols,
    in_sems, out_sems, part_send, part_recv, tot_send, tot_recv, proj_send, proj_recv,
    top_send, top_recv, sum_send, sum_recv, col_send, col_recv,
):
    row, rank = lax.axis_index("rows"), lax.axis_index("rank")
    everyone = n_rows * n_rank
    flat = row * n_rank + rank
    k, points = lp.shape
    ranks = k * n_rank
    tiles = points // LANES

    barrier = pltpu.get_barrier_semaphore()

    def place(other):
        return (other // n_rank, other % n_rank)

    def greet(step):
        pl.semaphore_signal(
            barrier, inc=1, device_id=place((flat + step) % everyone), device_id_type=MESH
        )

    each(1, everyone, greet)
    loads = []
    for index, (source, target) in enumerate(((lp_hbm, lp), (lf_hbm, lf), (rp_hbm, rp), (rf_hbm, rf))):
        load = pltpu.make_async_copy(source, target, in_sems.at[index])
        load.start()
        loads.append(load)

    def row_peer(step):
        return ((row + step) % n_rows, rank)

    def rank_peer(step):
        return (row, (rank + step) % n_rank)

    def flat_peer(step):
        return place((flat + step) % everyone)

    def copy(source, target, send, recv, device):
        return pltpu.make_async_remote_copy(
            src_ref=source, dst_ref=target, send_sem=send, recv_sem=recv,
            device_id=device, device_id_type=MESH,
        )

    def tile(ref, j):
        return ref[:, j * LANES : (j + 1) * LANES]

    for side, mass in enumerate((lm_ref, rm_ref)):
        total = tile(mass, 0)
        for j in range(1, tiles):
            total = total + tile(mass, j)
        totals[row, side : side + 1, :] = total
    log_row[:, :k] = log_ref[...]
    log_row[:, k:] = log_ref[...]

    def product(plan, factor):
        return lax.dot_general(
            plan[...].astype(jnp.bfloat16), factor[...], (((1,), (1,)), ((), ())),
            preferred_element_type=jnp.float32,
        )

    loads[0].wait()
    loads[1].wait()
    both = [product(lp, lf)]
    loads[2].wait()
    loads[3].wait()
    both.append(product(rp, rf))
    local = jnp.concatenate(both, axis=0)
    part[...] = local.reshape(part.shape)
    pl.semaphore_wait(barrier, everyone - 1)

    def part_copy(step):
        peer = (row + step) % n_rows
        return copy(part.at[peer], parts.at[row], part_send.at[step], part_recv.at[step], row_peer(step))

    def tot_copy(step):
        return copy(totals.at[row], totals.at[row], tot_send.at[step], tot_recv.at[step], row_peer(step))

    def proj_copy(step):
        return copy(proj.at[row], proj.at[row], proj_send.at[step], proj_recv.at[step], row_peer(step))

    each(1, n_rows, lambda step: part_copy(step).start())
    each(1, n_rows, lambda step: tot_copy(step).start())
    parts[row] = part[row]
    each(1, n_rows, lambda step: part_copy(step).wait_recv())
    proj[row] = jnp.sum(parts[...], axis=0)
    each(1, n_rows, lambda step: proj_copy(step).start())

    each(1, n_rows, lambda step: tot_copy(step).wait_recv())
    total = jnp.sum(jnp.sum(totals[...], axis=0), axis=1, keepdims=True)
    total_left, total_right = total[0:1], total[1:2]
    mean = total_left / ranks
    inner = mean * jnp.exp(log_row[...])
    inner_columns = to_columns(inner)
    norm = total_left / total_right
    mass_left = lm_ref[...]
    mass_right = rm_ref[...] * norm

    each(1, n_rows, lambda step: proj_copy(step).wait_recv())
    sums_all = proj[...].reshape(2 * k, LANES)
    scaled = (sums_all / inner_columns).astype(jnp.bfloat16)
    grads = []
    for scale, factor in ((scaled[k:], lf), (scaled[:k], rf)):
        grads.append(
            lax.dot_general(
                scale, factor[...], (((1,), (0,)), ((), ())), preferred_element_type=jnp.float32
            )
        )
    pair = scaled[k:].astype(jnp.float32) * sums_all[:k]
    pairing = jnp.sum(jnp.concatenate([pair, pair], axis=0).T, axis=0, keepdims=True)
    grad_inner = -pairing / inner
    peak = jnp.maximum(jnp.abs(grads[0]), jnp.abs(grads[1]))
    peak = jnp.max(peak, axis=0, keepdims=True)
    top = jnp.abs(grad_inner)
    for j in range(tiles):
        top = jnp.maximum(top, peak[:, j * LANES : (j + 1) * LANES])
    tops[flat] = top

    def top_copy(step):
        return copy(tops.at[flat], tops.at[flat], top_send.at[step], top_recv.at[step], flat_peer(step))

    each(1, everyone, lambda step: top_copy(step).start())
    each(1, everyone, lambda step: top_copy(step).wait_recv())
    largest = jnp.max(jnp.max(tops[...], axis=0), axis=1, keepdims=True)
    size = 5.0 / jnp.maximum(largest, 0.25)
    tilt[0] = lp[...] * jnp.exp(-size * grads[0])
    tilt[1] = rp[...] * jnp.exp(-size * grads[1])
    stores = []
    for side, target in enumerate((tl_hbm, tr_hbm)):
        store = pltpu.make_async_copy(tilt.at[side], target, out_sems.at[side])
        store.start()
        stores.append(store)
    log_inner = jnp.log(inner * jnp.exp(-size * grad_inner))
    col = jnp.ones_like(inner)
    columns = None

    for repeat in range(ITERS):
        def sum_copy(step):
            return copy(
                sums.at[repeat, rank], sums.at[repeat, rank],
                sum_send.at[repeat, step], sum_recv.at[repeat, step], rank_peer(step),
            )

        def col_copy(step):
            return copy(
                cols.at[repeat, row], cols.at[repeat, row],
                col_send.at[repeat, step], col_recv.at[repeat, step], row_peer(step),
            )

        for side in range(2):
            for j in range(tiles):
                lanes = slice(j * LANES, (j + 1) * LANES)
                block = tilt[side, :, lanes]
                if columns is not None:
                    block = block * columns[side * k : (side + 1) * k]
                sums[repeat, rank, side : side + 1, lanes] = jnp.sum(block, axis=0, keepdims=True)
        each(1, n_rank, lambda step: sum_copy(step).start())
        each(1, n_rank, lambda step: sum_copy(step).wait_recv())
        weight = jnp.sum(sums[repeat], axis=0)
        scales = (mass_left / weight[0:1], mass_right / weight[1:2])
        partial = []
        for side in range(2):
            acc = None
            for j in range(tiles):
                lanes = slice(j * LANES, (j + 1) * LANES)
                term = tilt[side, :, lanes] * scales[side][:, lanes]
                acc = term if acc is None else acc + term
            partial.append(acc)
        cols[repeat, row] = jnp.sum(jnp.concatenate(partial, axis=0).T, axis=0, keepdims=True)
        each(1, n_rows, lambda step: col_copy(step).start())
        if repeat == ITERS - 1:
            scale_ref[0:1, :] = scales[0]
            scale_ref[1:2, :] = scales[1]
        each(1, n_rows, lambda step: col_copy(step).wait_recv())
        total_col = jnp.sum(cols[repeat], axis=0)
        own = jnp.log(col * total_col)
        log_inner = (log_inner + own + pltpu.roll(own, k, 1)) / 3.0
        col = jnp.exp(log_inner) / total_col
        if repeat < ITERS - 1:
            columns = to_columns(col)
        each(1, n_rank, lambda step: sum_copy(step).wait_send())
        each(1, n_rows, lambda step: col_copy(step).wait_send())

    col_ref[...] = col
    log_out[...] = log_inner - jnp.log(mean)
    each(1, n_rows, lambda step: part_copy(step).wait_send())
    each(1, n_rows, lambda step: tot_copy(step).wait_send())
    each(1, n_rows, lambda step: proj_copy(step).wait_send())
    each(1, everyone, lambda step: top_copy(step).wait_send())
    for store in stores:
        store.wait()


def solution(mesh):
    n_rows, n_rank = mesh.shape["rows"], mesh.shape["rank"]
    everyone = n_rows * n_rank

    def per_device(left_factor, right_factor, left_plan, right_plan, log_inner, left_mass, right_mass):
        k, points = left_plan.shape
        depth = left_factor.shape[0]
        lines = 2 * k // n_rows
        f32 = jnp.float32
        whole = pl.BlockSpec(memory_space=pl.ANY)
        near = pl.BlockSpec(memory_space=pltpu.VMEM)
        dma = pltpu.SemaphoreType.DMA
        tilted_left, tilted_right, row_scale, col_scale, new_log = pl.pallas_call(
            functools.partial(kernel, n_rows, n_rank),
            out_shape=(
                jax.ShapeDtypeStruct((k, points), f32),
                jax.ShapeDtypeStruct((k, points), f32),
                jax.ShapeDtypeStruct((2, points), f32),
                jax.ShapeDtypeStruct((1, 2 * k), f32),
                jax.ShapeDtypeStruct((1, 2 * k), f32),
            ),
            in_specs=[whole] * 4 + [near] * 3,
            out_specs=(whole, whole, near, near, near),
            scratch_shapes=[
                pltpu.VMEM((depth, points), jnp.bfloat16),
                pltpu.VMEM((depth, points), jnp.bfloat16),
                pltpu.VMEM((k, points), f32),
                pltpu.VMEM((k, points), f32),
                pltpu.VMEM((2, k, points), f32),
                pltpu.VMEM((1, 2 * k), f32),
                pltpu.VMEM((n_rows, lines, depth), f32),
                pltpu.VMEM((n_rows, lines, depth), f32),
                pltpu.VMEM((lines, depth), f32),
                pltpu.VMEM((n_rows, lines, depth), f32),
                pltpu.VMEM((n_rows, 2, LANES), f32),
                pltpu.VMEM((everyone, 1, LANES), f32),
                pltpu.VMEM((ITERS, n_rank, 2, points), f32),
                pltpu.VMEM((ITERS, n_rows, 1, 2 * k), f32),
                dma((4,)),
                dma((2,)),
                dma((n_rows,)),
                dma((n_rows,)),
                dma((n_rows,)),
                dma((n_rows,)),
                dma((n_rows,)),
                dma((n_rows,)),
                dma((everyone,)),
                dma((everyone,)),
                dma((ITERS, n_rank)),
                dma((ITERS, n_rank)),
                dma((ITERS, n_rows)),
                dma((ITERS, n_rows)),
            ],
            compiler_params=pltpu.CompilerParams(collective_id=0, has_side_effects=True),
        )(
            left_factor, right_factor, left_plan, right_plan,
            log_inner[None, :], left_mass[None, :], right_mass[None, :],
        )
        new_left = row_scale[0][None, :] * tilted_left * col_scale[0, :k][:, None]
        new_right = row_scale[1][None, :] * tilted_right * col_scale[0, k:][:, None]
        return new_left, new_right, new_log[0, :k]

    in_specs = (
        P(None, "rows"),
        P(None, "rows"),
        P("rank", "rows"),
        P("rank", "rows"),
        P("rank"),
        P("rows"),
        P("rows"),
    )
    out_specs = (P("rank", "rows"), P("rank", "rows"), P("rank"))
    return jax.shard_map(
        per_device, mesh=mesh, in_specs=in_specs, out_specs=out_specs, check_vma=False
    )
```

time: 223 us -> 50.5 us (0.23)
  blocking collectives: 201 us -> 0 us
  Pallas kernels: 0 us -> 44.9 us
  matrix products: 9.56 us -> 0 us
  between operations: 5.5 us -> 0.65 us
  other arithmetic: 6.36 us -> 2.3 us
    psum x8 -> x0, blocking collectives: 164 us -> none  [the longest x2 75.7 us: per_device(): lax.psum((contract_points(right_factor, right_round), contract_points(lef...]
    pallas_call x0 -> x1, Pallas kernels: none -> 44.9 us  [per_device(): pl.pallas_call(functools.partial(kernel, n_rows, n_rank), out_shape=(jax....]
    pmax x1 -> x0, blocking collectives: 36.8 us -> none  [per_device(): largest = lax.pmax(local_top, ('rows', 'rank'))]
    dot_general x16 -> x0, matrix products: 9.56 us -> none  [the longest x2 2.52 us: expand_points(): lax.dot_general(projected, factor, (((0,), (0,)), ((), ())), preferred_el...]
where the time goes in v1:
time: 50.5 us; the launch traced here: 50 us
  Pallas kernels  44.9 us (89%)
  other arithmetic  2.3 us (5%)
  local copies, waits for them, and re-layouts  2.16 us (4%)
  between operations  0.65 us (1%)
    pallas_call x1, Pallas kernels, per_device(): pl.pallas_call(functools.partial(kernel, n_rows, n_rank), out_shape=(jax....  44.9 us
    mul x1, other arithmetic, per_device(): new_right = row_scale[1][None, :] * tilted_right * col_scale[0, k:][:, None]  2.3 us

profile of v1, /device:TPU:0, one launch (start us, length us, event | category | flops | bytes accessed | tf_op | source)
XLA Modules:
  0.0 50.0 jit_solution(13596190182552637566)
XLA Ops:
  0.6 44.9 %shard_map.94 = (f32[64,2048]{1,0:T(8,128)}, f32[64,2048]{1,0:T(8,128)}, f32[2,2048]{1,0:T(2,128)}, f32[1,128]{1,0:T(1,128)}, f32[1,128]{1,0:T(1,128)}) custom-call(bf16[128,2048]{1,0:T(8,128)(2,1)} %lf_hbm.1, bf16[128,2048]{1,0:T(8,128)(2,1)} %rf_hbm.1, f32[64,2048]{1,0:T(8,128)} %lp_hbm.1, f32[64,2048]{1,0:T(8,128)} %rp_hbm.1, f32[1,64]{1,0:T(1,128)} %bitcast.15, ...), custom_call_target="tpu_custom_call" | custom-call | tf_op jit(solution)/shard_map/pallas_call | solution.py:237
  45.6 0.8 %fusion = (f32[1,2048]{1,0:T(1,128)S(1)}, f32[1,2048]{1,0:T(1,128)S(1)}) fusion(f32[2,2048]{1,0:T(2,128)} %get-tuple-element.8), kind=kLoop, calls=%fused_computation.5 | loop fusion | bytes 32768 | tf_op jit(solution)/shard_map/slice | solution.py:284
  46.4 0.0 copy-start.1
  46.4 0.7 %copy-done.1 = f32[1,128]{1,0:T(1,128)S(1)} copy-done((f32[1,128]{1,0:T(1,128)S(1)}, f32[1,128]{1,0:T(1,128)}, u32[]{:S(2)}) %copy-start.1) | copy-done | bytes 536
  47.0 0.0 copy-start
  47.0 0.5 %slice_bitcast_fusion = f32[64]{0:T(128)} fusion(f32[1,128]{1,0:T(1,128)S(1)} %copy-done.1), kind=kLoop, calls=%fused_computation.2 | loop fusion | bytes 512 | tf_op jit(solution)/shard_map/squeeze | solution.py:285
  47.5 0.1 copy-done
  47.7 0.1 slice_bitcast_fusion.1
  47.7 2.3 %multiply_multiply_fusion = (f32[64,2048]{1,0:T(8,128)}, f32[64,2048]{1,0:T(8,128)}) fusion(f32[64,2048]{1,0:T(8,128)} %get-tuple-element.11, f32[64]{0:T(128)S(1)} %get-tuple-element.15, f32[2048]{0:T(1024)S(1)} %bitcast.11, f32[64]{0:T(128)S(1)} %get-tuple-element.16, f32[64,2048]{1,0:T(8,128)} %get-tuple-element.9, f32[2048]{0:T(1024)S(1)} %bitcast.12), kind=kLoop, calls=%fused_computation | loop fusion | flops 524288 | bytes 2114048 | tf_op jit(solution)/shard_map/mul | solution.py:284
Async XLA Ops:
  46.4 0.7 %copy-start.1 = (f32[1,128]{1,0:T(1,128)S(1)}, f32[1,128]{1,0:T(1,128)}, u32[]{:S(2)}) copy-start(f32[1,128]{1,0:T(1,128)} %get-tuple-element.12) | copy-start | bytes 1540
  47.0 0.6 %copy-start = (f32[1,128]{1,0:T(1,128)S(1)}, f32[1,128]{1,0:T(1,128)}, u32[]{:S(2)}) copy-start(f32[1,128]{1,0:T(1,128)} %get-tuple-element.10) | copy-start | bytes 1540
